TPU v7x, 32 devices: a whole 2x2x4 slice. The times are simulated.
32 devices in a mesh: img: 2 (over x), ga: 4 (over y, core), band: 4 (over z).
Axes of the slice: x: 2, y: 2, z: 4, core: 2. Of those that a mesh axis runs over, the one named last changes fastest.
Arguments:
- orbitals: bfloat16 [1536, 12288], P(('img', 'band'), 'ga'), parts along dimension 0, as said below
- kernel: float32 [12288], P('ga'), may hold values from 0.3 to 3
- block_vectors: bfloat16 [512, 12288], P(('img', 'band'), 'ga'), parts along dimension 0
Outputs:
- ace_vectors: bfloat16 [1536, 12288], P(('img', 'band'), 'ga'), parts along dimension 0
- exchange_block: bfloat16 [512, 12288], P(('img', 'band'), 'ga'), parts along dimension 0
There are 2 independent parts, one for each index of `img`. A program takes and returns all parts, laid end to end along the dimension named above; an argument that names none is the same for every part. Nothing has to cross between parts.
Inputs may be any that keep to these rules, and one draw needn't show every extreme that they name: `orbitals`: the bands of one image are linearly independent, and the block lies largely in their span.
All inputs are finite; a program needn't handle non-finite values.
Results may differ from a plain program's by a relative error of at most 0.02.
Values may be sent and summed in bfloat16 or wider, within the bound.
A program may use at most 64 MiB of HBM per device.

v0:
```python
import jax
import jax.numpy as jnp
from jax import lax
from jax.sharding import PartitionSpec as P


def contract_first(left, right):
    return lax.dot_general(left, right, (((0,), (0,)), ((), ())), precision=lax.Precision.HIGHEST)


def shards(orbitals, kernel, block_vectors):
    groups = lax.axis_size("ga")
    own_band = lax.axis_index("band")
    total_coeffs = orbitals.shape[1] * groups
    full_orbitals, full_block = (
        lax.all_gather(orbitals, "band", axis=0, tiled=True),
        lax.all_gather(block_vectors, "band", axis=0, tiled=True),
    )
    weighted = (-(full_orbitals.astype(jnp.float32) * kernel[None, :])).astype(jnp.bfloat16)
    own_rows = orbitals.shape[0]
    partial_rows = lax.dot_general(
        orbitals, weighted, (((1,), (1,)), ((), ())), preferred_element_type=jnp.float32
    )
    summed_rows = lax.psum(partial_rows.astype(jnp.bfloat16), "ga").astype(jnp.float32)
    margin = -lax.all_gather(summed_rows, "band", axis=0, tiled=True) / total_coeffs
    factor = jnp.linalg.cholesky(margin)
    identity = jnp.eye(factor.shape[0], dtype=jnp.float32)
    inverse = lax.linalg.triangular_solve(factor, identity, left_side=True, lower=True)
    inverse_rows = lax.dynamic_slice_in_dim(inverse, own_band * own_rows, own_rows, 0)
    projector = jnp.dot(inverse_rows, weighted.astype(jnp.float32), precision=lax.Precision.HIGHEST)
    local_coupling = jnp.dot(
        projector, full_block.astype(jnp.float32).T, precision=lax.Precision.HIGHEST
    )
    coupling = (
        lax.psum(local_coupling.astype(jnp.bfloat16), "ga").astype(jnp.float32) / total_coeffs
    )
    applied = lax.psum_scatter(
        -contract_first(coupling, projector), "band", scatter_dimension=0, tiled=True
    )
    return (projector.astype(jnp.bfloat16), applied.astype(jnp.bfloat16))


def solution(mesh):
    placed = (P(("img", "band"), "ga"), P("ga"), P(("img", "band"), "ga"))
    return jax.shard_map(
        shards,
        mesh=mesh,
        in_specs=placed,
        out_specs=(P(("img", "band"), "ga"), P(("img", "band"), "ga")),
        check_vma=False,
    )
```

profile of v0, /device:TPU:0, one launch (start us, length us, event | category | flops | bytes accessed | tf_op | source)
XLA Modules:
  0.0 548.5 jit_solution(6717364289099904385)
XLA Ops:
  7.9 93.7 %all-gather.4.cloned.1.call-done = bf16[768,3072]{1,0:T(8,128)(2,1)} async-done(((bf16[192,3072]{1,0:T(8,128)(2,1)}), bf16[768,3072]{1,0:T(8,128)(2,1)}) %all-gather.4.cloned.1.call-update) | async-done | bytes 4718608 | tf_op jit(solution)/shard_map/all_gather | solution.py:16
  101.7 5.1 fusion.20
  106.9 30.9 %all-reduce.4.cloned.1.call-done = bf16[192,768]{1,0:T(8,128)(2,1)} async-done(((bf16[192,768]{1,0:T(8,128)(2,1)}), bf16[192,768]{1,0:T(8,128)(2,1)}) %all-reduce.4.cloned.1.call-update) | async-done | bytes 294928 | tf_op jit(solution)/shard_map/psum | solution.py:24
  142.1 47.9 %all-gather.6.cloned.1.call-done = f32[768,768]{1,0:T(8,128)} async-done(((f32[192,768]{1,0:T(8,128)}), f32[768,768]{1,0:T(8,128)}) %all-gather.6.cloned.1.call-update) | async-done | bytes 2359312 | tf_op jit(solution)/shard_map/all_gather | solution.py:25
  190.0 2.0 copy.7
  193.7 3.2 copy.8
  197.0 2.1 fusion.2
  200.5 11.7 %cholesky.165 = f32[128,128]{1,0:T(8,128)S(1)} custom-call(f32[128,128]{1,0:T(8,128)S(1)} %cholesky.424), custom_call_target="Cholesky" | custom-call | tf_op jit(solution)/shard_map/jit(cholesky)/cholesky | solution.py:26
  212.3 9.8 %custom-call.46 = f32[1,128,128]{1,2,0:T(8,128)S(1)} custom-call(f32[1,128,128]{2,1,0:T(8,128)S(1)} %get-tuple-element.45), custom_call_target="InvertDiagBlocksLowerTriangular" | custom-call | tf_op jit(solution)/shard_map/jit(cholesky)/cholesky | solution.py:26
  225.0 11.7 %cholesky.188 = f32[128,128]{1,0:T(8,128)S(1)} custom-call(f32[128,128]{1,0:T(8,128)S(1)} %cholesky.428), custom_call_target="Cholesky" | custom-call | tf_op jit(solution)/shard_map/jit(cholesky)/cholesky | solution.py:26
  236.8 10.0 %custom-call.47 = f32[1,128,128]{1,2,0:T(8,128)S(1)} custom-call(f32[1,128,128]{2,1,0:T(8,128)S(1)} %get-tuple-element.42), custom_call_target="InvertDiagBlocksLowerTriangular" | custom-call | tf_op jit(solution)/shard_map/jit(cholesky)/cholesky | solution.py:26
  248.7 11.7 %cholesky.354 = f32[128,128]{1,0:T(8,128)S(1)} custom-call(f32[128,128]{1,0:T(8,128)S(1)} %cholesky.433), custom_call_target="Cholesky" | custom-call | tf_op jit(solution)/shard_map/jit(cholesky)/cholesky | solution.py:26
  261.2 9.8 %custom-call.48 = f32[1,128,128]{1,2,0:T(8,128)S(1)} custom-call(f32[1,128,128]{2,1,0:T(8,128)S(1)} %get-tuple-element.39), custom_call_target="InvertDiagBlocksLowerTriangular" | custom-call | tf_op jit(solution)/shard_map/jit(cholesky)/cholesky | solution.py:26
  272.9 12.2 %cholesky.373 = f32[128,128]{1,0:T(8,128)S(1)} custom-call(f32[128,128]{1,0:T(8,128)S(1)} %cholesky.438), custom_call_target="Cholesky" | custom-call | tf_op jit(solution)/shard_map/jit(cholesky)/cholesky | solution.py:26
  285.8 9.8 %custom-call.49 = f32[1,128,128]{1,2,0:T(8,128)S(1)} custom-call(f32[1,128,128]{2,1,0:T(8,128)S(1)} %get-tuple-element.36), custom_call_target="InvertDiagBlocksLowerTriangular" | custom-call | tf_op jit(solution)/shard_map/jit(cholesky)/cholesky | solution.py:26
  297.4 11.7 %cholesky.392 = f32[128,128]{1,0:T(8,128)S(1)} custom-call(f32[128,128]{1,0:T(8,128)S(1)} %cholesky.443), custom_call_target="Cholesky" | custom-call | tf_op jit(solution)/shard_map/jit(cholesky)/cholesky | solution.py:26
  309.8 9.8 %custom-call.50 = f32[1,128,128]{1,2,0:T(8,128)S(1)} custom-call(f32[1,128,128]{2,1,0:T(8,128)S(1)} %get-tuple-element.33), custom_call_target="InvertDiagBlocksLowerTriangular" | custom-call | tf_op jit(solution)/shard_map/jit(cholesky)/cholesky | solution.py:26
  321.2 11.9 %cholesky.410 = f32[128,128]{1,0:T(8,128)S(1)} custom-call(f32[128,128]{1,0:T(8,128)S(1)} %convolution_subtract_fusion.8), custom_call_target="Cholesky" | custom-call | tf_op jit(solution)/shard_map/jit(cholesky)/cholesky | solution.py:26
  340.0 21.3 %while.1 = (s32[]{:T(128)}, f32[768,768]{1,0:T(8,128)}, s32[6,2]{0,1:T(2,128)S(1)}, f32[6,128,128]{2,1,0:T(8,128)}, s32[]{:T(128)}) while((s32[]{:T(128)}, f32[768,768]{1,0:T(8,128)}, s32[6,2]{0,1:T(2,128)S(1)}, f32[6,128,128]{2,1,0:T(8,128)}, s32[]{:T(128)}) %tuple.45), condition=%wide.while_cond, body=%wide.while_body.sunk | while | flops 2 | bytes 132705 | solution.py:28
  340.6 3.0 bitcast_dynamic-update-slice_fusion.2
  344.3 2.9 bitcast_dynamic-update-slice_fusion.2
  347.8 2.9 bitcast_dynamic-update-slice_fusion.2
  351.4 2.9 bitcast_dynamic-update-slice_fusion.2
  354.9 2.9 bitcast_dynamic-update-slice_fusion.2
  358.4 2.8 bitcast_dynamic-update-slice_fusion.2
  361.3 60.4 %custom-call.51 = f32[6,128,128]{1,2,0:T(8,128)} custom-call(f32[6,128,128]{2,1,0:T(8,128)} %get-tuple-element.9), custom_call_target="InvertDiagBlocksLowerTriangular" | custom-call | tf_op jit(solution)/shard_map/triangular_solve | solution.py:28
  432.2 2.3 convolution_subtract_fusion
  435.0 4.2 fusion.65
  439.3 3.8 convolution_convert_fusion
  443.4 30.3 %all-reduce.6.cloned.1.call-done = bf16[192,256]{1,0:T(8,128)(2,1)} async-done(((bf16[192,256]{1,0:T(8,128)(2,1)}), bf16[192,256]{1,0:T(8,128)(2,1)}) %all-reduce.6.cloned.1.call-update) | async-done | bytes 98320 | tf_op jit(solution)/shard_map/psum | solution.py:35
  473.6 5.3 convolution_negate_fusion
  479.0 60.6 %reduce-scatter.2.cloned.1.call-done = f32[64,3072]{1,0:T(8,128)} async-done(((f32[256,3072]{1,0:T(8,128)}), f32[64,3072]{1,0:T(8,128)}) %reduce-scatter.2.cloned.1.call-update) | async-done | bytes 786448 | tf_op jit(solution)/shard_map/reduce_scatter | solution.py:37
  (84 shorter events, 40.5 us)
Async XLA Ops:
  7.2 94.5 %all-gather.4.cloned.1.call-start = ((), (), s32[]{:S(2)}) async-start(), calls=%async_computation.1 | async-start | bytes 5898240 | tf_op jit(solution)/shard_map/all_gather | solution.py:16
  7.9 130.0 %all-reduce.4.cloned.1.call-start = ((), (), s32[]{:S(2)}) async-start(), calls=%async_computation.2 | async-start | bytes 589824 | tf_op jit(solution)/shard_map/psum | solution.py:24
  106.9 83.2 %all-gather.6.cloned.1.call-start = ((), (), s32[]{:S(2)}) async-start(), calls=%async_computation.3 | async-start | bytes 2949120 | tf_op jit(solution)/shard_map/all_gather | solution.py:25
  139.7 299.6 %all-gather.8.cloned.1.call-start = ((), (), s32[]{:S(2)}) async-start(), calls=%async_computation.4 | async-start | bytes 1966080 | tf_op jit(solution)/shard_map/all_gather | solution.py:17
  140.3 333.4 %all-reduce.6.cloned.1.call-start = ((), (), s32[]{:S(2)}) async-start(), calls=%async_computation.5 | async-start | bytes 196608 | tf_op jit(solution)/shard_map/psum | solution.py:35
  199.0 1.5 copy-start.1
  340.0 85.0 %copy-start = (f32[768,768]{1,0:T(8,128)S(1)}, f32[768,768]{1,0:T(8,128)}, u32[]{:S(2)}) copy-start(f32[768,768]{1,0:T(8,128)} %fusion.24) | copy-start | bytes 7077892
  421.7 2.8 copy-start.2
  427.1 7.9 %slice-start = ((s8[4718592]{0:T(1024)(128)(4,1)}), s8[4194304]{0:T(1024)(128)(4,1)S(1)}, s32[]{:S(2)}) async-start(s8[4718592]{0:T(1024)(128)(4,1)} %bitcast.83), calls=%async_computation.7 | async-start | bytes 8388608
  429.6 5.4 slice-start.1
  431.6 3.4 copy-start.3
  443.1 96.4 %reduce-scatter.2.cloned.1.call-start = ((), (), s32[]{:S(2)}) async-start(), calls=%async_computation.6 | async-start | bytes 3932160 | tf_op jit(solution)/shard_map/reduce_scatter | solution.py:37
Sparse Core Ops, SparseCore 0:
  9.5 92.1 all-gather.3
  107.0 30.8 all-reduce.3
  140.0 49.9 all-gather.5
  191.4 35.7 all-gather.7
  443.2 30.3 all-reduce.5
  479.1 60.3 reduce-scatter.1
where the time goes:
time: 552 us; the launch traced here: 549 us
  waiting for transfers between devices  265 us (48%)
  other arithmetic  195 us (35%)
  matrix products  41.5 us (8%)
  local copies, waits for them, and re-layouts  28.2 us (5%)
  between operations  18.6 us (3%)
    another operation x22, other arithmetic, shards(): factor = jnp.linalg.cholesky(margin)  124 us
    all_gather x1, waiting for transfers between devices, shards(): lax.all_gather(orbitals, 'band', axis=0, tiled=True)  93.7 us
    another operation x3, other arithmetic, shards(): lax.linalg.triangular_solve(factor, identity, left_side=True, lower=True)  62 us
    reduce_scatter x1, waiting for transfers between devices, shards(): lax.psum_scatter(-contract_first(coupling, projector), 'band', scatter_di...  60.6 us
    all_gather x1, waiting for transfers between devices, shards(): lax.all_gather(summed_rows, 'band', axis=0, tiled=True)  47.9 us
    psum x1, waiting for transfers between devices, shards(): lax.psum(partial_rows.astype(jnp.bfloat16), 'ga').astype(jnp.float32)  30.9 us
    psum x1, waiting for transfers between devices, shards(): lax.psum(local_coupling.astype(jnp.bfloat16), 'ga').astype(jnp.float32)  30.3 us
    another operation x18, local copies, waits for them, and re-layouts  21.3 us
  transfers between devices with their start and end apart: 6, of which 5 were waited for; matrix products, arithmetic and copies ran while one was open for 45% of the time, Pallas kernels for 0%

commit v1 on v0

--- a/solution.py
+++ b/solution.py
@@ -32,7 +32,10 @@
         projector, full_block.astype(jnp.float32).T, precision=lax.Precision.HIGHEST
     )
     coupling = (
-        lax.psum(local_coupling.astype(jnp.bfloat16), "ga").astype(jnp.float32) / total_coeffs
+        jnp.sum(lax.all_gather(local_coupling.astype(jnp.bfloat16), "ga"), axis=0).astype(
+            jnp.float32
+        )
+        / total_coeffs
     )
     applied = lax.psum_scatter(
         -contract_first(coupling, projector), "band", scatter_dimension=0, tiled=True

time: 552 us -> 525 us (0.951)
  waiting for transfers between devices: 265 us -> 233 us
  blocking collectives: 0 us -> 6.69 us
    psum x1 -> x0, waiting for transfers between devices: 30.3 us -> none  [shards(): lax.psum(local_coupling.astype(jnp.bfloat16), 'ga').astype(jnp.float32)]
    all_gather x0 -> x1, blocking collectives: none -> 6.69 us  [shards(): lax.all_gather(local_coupling.astype(jnp.bfloat16), 'ga')]
  transfers between devices with their start and end apart: 6 -> 5, of which waited for: 5 -> 4; matrix products, arithmetic and copies ran while one was open for 45% -> 47% of each run, Pallas kernels for 0% -> 0%
where the time goes in v1:
time: 525 us; the launch traced here: 521 us
  waiting for transfers between devices  233 us (44%)
  other arithmetic  195 us (37%)
  matrix products  39.9 us (8%)
  local copies, waits for them, and re-layouts  28.2 us (5%)
  between operations  18.3 us (3%)
  blocking collectives  6.69 us (1%)
    another operation x22, other arithmetic, shards(): factor = jnp.linalg.cholesky(margin)  124 us
    all_gather x1, waiting for transfers between devices, shards(): lax.all_gather(orbitals, 'band', axis=0, tiled=True)  93.7 us
    another operation x3, other arithmetic, shards(): lax.linalg.triangular_solve(factor, identity, left_side=True, lower=True)  62 us
    reduce_scatter x1, waiting for transfers between devices, shards(): lax.psum_scatter(-contract_first(coupling, projector), 'band', scatter_di...  59 us
    all_gather x1, waiting for transfers between devices, shards(): lax.all_gather(summed_rows, 'band', axis=0, tiled=True)  47.9 us
    psum x1, waiting for transfers between devices, shards(): lax.psum(partial_rows.astype(jnp.bfloat16), 'ga').astype(jnp.float32)  30.9 us
    another operation x18, local copies, waits for them, and re-layouts  21.3 us
    another operation x11, matrix products, shards(): lax.linalg.triangular_solve(factor, identity, left_side=True, lower=True)  13.2 us
  transfers between devices with their start and end apart: 5, of which 4 were waited for; matrix products, arithmetic and copies ran while one was open for 47% of the time, Pallas kernels for 0%

profile of v1, /device:TPU:0, one launch (start us, length us, event | category | flops | bytes accessed | tf_op | source)
XLA Modules:
  0.0 521.3 jit_solution(18054667933917096453)
XLA Ops:
  7.9 93.7 %all-gather.5.cloned.1.call-done = bf16[768,3072]{1,0:T(8,128)(2,1)} async-done(((bf16[192,3072]{1,0:T(8,128)(2,1)}), bf16[768,3072]{1,0:T(8,128)(2,1)}) %all-gather.5.cloned.1.call-update) | async-done | bytes 4718608 | tf_op jit(solution)/shard_map/all_gather | solution.py:16
  101.7 5.1 fusion.20
  106.9 30.9 %all-reduce.3.cloned.1.call-done = bf16[192,768]{1,0:T(8,128)(2,1)} async-done(((bf16[192,768]{1,0:T(8,128)(2,1)}), bf16[192,768]{1,0:T(8,128)(2,1)}) %all-reduce.3.cloned.1.call-update) | async-done | bytes 294928 | tf_op jit(solution)/shard_map/psum | solution.py:24
  142.1 47.9 %all-gather.7.cloned.1.call-done = f32[768,768]{1,0:T(8,128)} async-done(((f32[192,768]{1,0:T(8,128)}), f32[768,768]{1,0:T(8,128)}) %all-gather.7.cloned.1.call-update) | async-done | bytes 2359312 | tf_op jit(solution)/shard_map/all_gather | solution.py:25
  190.0 2.0 copy.7
  193.7 3.2 copy.8
  197.0 2.1 fusion.2
  200.5 11.7 %cholesky.165 = f32[128,128]{1,0:T(8,128)S(1)} custom-call(f32[128,128]{1,0:T(8,128)S(1)} %cholesky.424), custom_call_target="Cholesky" | custom-call | tf_op jit(solution)/shard_map/jit(cholesky)/cholesky | solution.py:26
  212.3 9.8 %custom-call.46 = f32[1,128,128]{1,2,0:T(8,128)S(1)} custom-call(f32[1,128,128]{2,1,0:T(8,128)S(1)} %get-tuple-element.45), custom_call_target="InvertDiagBlocksLowerTriangular" | custom-call | tf_op jit(solution)/shard_map/jit(cholesky)/cholesky | solution.py:26
  225.0 11.7 %cholesky.188 = f32[128,128]{1,0:T(8,128)S(1)} custom-call(f32[128,128]{1,0:T(8,128)S(1)} %cholesky.428), custom_call_target="Cholesky" | custom-call | tf_op jit(solution)/shard_map/jit(cholesky)/cholesky | solution.py:26
  236.8 10.0 %custom-call.47 = f32[1,128,128]{1,2,0:T(8,128)S(1)} custom-call(f32[1,128,128]{2,1,0:T(8,128)S(1)} %get-tuple-element.42), custom_call_target="InvertDiagBlocksLowerTriangular" | custom-call | tf_op jit(solution)/shard_map/jit(cholesky)/cholesky | solution.py:26
  248.7 11.7 %cholesky.354 = f32[128,128]{1,0:T(8,128)S(1)} custom-call(f32[128,128]{1,0:T(8,128)S(1)} %cholesky.433), custom_call_target="Cholesky" | custom-call | tf_op jit(solution)/shard_map/jit(cholesky)/cholesky | solution.py:26
  261.2 9.8 %custom-call.48 = f32[1,128,128]{1,2,0:T(8,128)S(1)} custom-call(f32[1,128,128]{2,1,0:T(8,128)S(1)} %get-tuple-element.39), custom_call_target="InvertDiagBlocksLowerTriangular" | custom-call | tf_op jit(solution)/shard_map/jit(cholesky)/cholesky | solution.py:26
  272.9 12.2 %cholesky.373 = f32[128,128]{1,0:T(8,128)S(1)} custom-call(f32[128,128]{1,0:T(8,128)S(1)} %cholesky.438), custom_call_target="Cholesky" | custom-call | tf_op jit(solution)/shard_map/jit(cholesky)/cholesky | solution.py:26
  285.8 9.8 %custom-call.49 = f32[1,128,128]{1,2,0:T(8,128)S(1)} custom-call(f32[1,128,128]{2,1,0:T(8,128)S(1)} %get-tuple-element.36), custom_call_target="InvertDiagBlocksLowerTriangular" | custom-call | tf_op jit(solution)/shard_map/jit(cholesky)/cholesky | solution.py:26
  297.4 11.7 %cholesky.392 = f32[128,128]{1,0:T(8,128)S(1)} custom-call(f32[128,128]{1,0:T(8,128)S(1)} %cholesky.443), custom_call_target="Cholesky" | custom-call | tf_op jit(solution)/shard_map/jit(cholesky)/cholesky | solution.py:26
  309.8 9.8 %custom-call.50 = f32[1,128,128]{1,2,0:T(8,128)S(1)} custom-call(f32[1,128,128]{2,1,0:T(8,128)S(1)} %get-tuple-element.33), custom_call_target="InvertDiagBlocksLowerTriangular" | custom-call | tf_op jit(solution)/shard_map/jit(cholesky)/cholesky | solution.py:26
  321.2 11.9 %cholesky.410 = f32[128,128]{1,0:T(8,128)S(1)} custom-call(f32[128,128]{1,0:T(8,128)S(1)} %convolution_subtract_fusion.8), custom_call_target="Cholesky" | custom-call | tf_op jit(solution)/shard_map/jit(cholesky)/cholesky | solution.py:26
  340.0 21.3 %while.1 = (s32[]{:T(128)}, f32[768,768]{1,0:T(8,128)}, s32[6,2]{0,1:T(2,128)S(1)}, f32[6,128,128]{2,1,0:T(8,128)}, s32[]{:T(128)}) while((s32[]{:T(128)}, f32[768,768]{1,0:T(8,128)}, s32[6,2]{0,1:T(2,128)S(1)}, f32[6,128,128]{2,1,0:T(8,128)}, s32[]{:T(128)}) %tuple.45), condition=%wide.while_cond, body=%wide.while_body.sunk | while | flops 2 | bytes 132705 | solution.py:28
  340.6 3.0 bitcast_dynamic-update-slice_fusion.2
  344.3 2.9 bitcast_dynamic-update-slice_fusion.2
  347.8 2.9 bitcast_dynamic-update-slice_fusion.2
  351.4 2.9 bitcast_dynamic-update-slice_fusion.2
  354.9 2.9 bitcast_dynamic-update-slice_fusion.2
  358.4 2.8 bitcast_dynamic-update-slice_fusion.2
  361.3 60.4 %custom-call.51 = f32[6,128,128]{1,2,0:T(8,128)} custom-call(f32[6,128,128]{2,1,0:T(8,128)} %get-tuple-element.9), custom_call_target="InvertDiagBlocksLowerTriangular" | custom-call | tf_op jit(solution)/shard_map/triangular_solve | solution.py:28
  432.2 2.3 convolution_subtract_fusion
  435.0 4.2 fusion.65
  439.3 3.2 convolution_convert_fusion
  442.4 6.7 %all-gather = bf16[768,256]{1,0:T(8,128)(2,1)S(1)} all-gather(bf16[192,256]{1,0:T(8,128)(2,1)S(1)} %convolution_convert_fusion), channel_id=2, replica_groups=mesh['img'=2,'ga'=4,'band'=4] {'ga'}, dimensions={0}, use_global_device_ids=true | all-gather | bytes 491520 | tf_op jit(solution)/shard_map/all_gather | solution.py:35
  449.2 4.4 convolution_negate_fusion
  453.6 59.0 %reduce-scatter.2.cloned.1.call-done = f32[64,3072]{1,0:T(8,128)} async-done(((f32[256,3072]{1,0:T(8,128)}), f32[64,3072]{1,0:T(8,128)}) %reduce-scatter.2.cloned.1.call-update) | async-done | bytes 786448 | tf_op jit(solution)/shard_map/reduce_scatter | solution.py:40
  (83 shorter events, 40.3 us)
Async XLA Ops:
  7.2 94.5 %all-gather.5.cloned.1.call-start = ((), (), s32[]{:S(2)}) async-start(), calls=%async_computation.1 | async-start | bytes 5898240 | tf_op jit(solution)/shard_map/all_gather | solution.py:16
  7.9 130.0 %all-reduce.3.cloned.1.call-start = ((), (), s32[]{:S(2)}) async-start(), calls=%async_computation.2 | async-start | bytes 589824 | tf_op jit(solution)/shard_map/psum | solution.py:24
  106.9 83.2 %all-gather.7.cloned.1.call-start = ((), (), s32[]{:S(2)}) async-start(), calls=%async_computation.3 | async-start | bytes 2949120 | tf_op jit(solution)/shard_map/all_gather | solution.py:25
  139.7 299.6 %all-gather.9.cloned.1.call-start = ((), (), s32[]{:S(2)}) async-start(), calls=%async_computation.4 | async-start | bytes 1966080 | tf_op jit(solution)/shard_map/all_gather | solution.py:17
  140.3 372.3 %reduce-scatter.2.cloned.1.call-start = ((), (), s32[]{:S(2)}) async-start(), calls=%async_computation.5 | async-start | bytes 3932160 | tf_op jit(solution)/shard_map/reduce_scatter | solution.py:40
  199.0 1.5 copy-start.1
  340.0 85.0 %copy-start = (f32[768,768]{1,0:T(8,128)S(1)}, f32[768,768]{1,0:T(8,128)}, u32[]{:S(2)}) copy-start(f32[768,768]{1,0:T(8,128)} %fusion.24) | copy-start | bytes 7077892
  421.7 2.8 copy-start.2
  427.1 7.9 %slice-start = ((s8[4718592]{0:T(1024)(128)(4,1)}), s8[4194304]{0:T(1024)(128)(4,1)S(1)}, s32[]{:S(2)}) async-start(s8[4718592]{0:T(1024)(128)(4,1)} %bitcast.85), calls=%async_computation.6 | async-start | bytes 8388608
  429.6 5.4 %slice-start.1 = ((s8[4718592]{0:T(1024)(128)(4,1)}), s8[524288]{0:T(1024)(128)(4,1)S(1)}, s32[]{:S(2)}) async-start(s8[4718592]{0:T(1024)(128)(4,1)} %bitcast.85), calls=%async_computation.7 | async-start | bytes 1048576
  431.6 3.4 copy-start.3
Sparse Core Ops, SparseCore 0:
  9.5 92.1 all-gather.4
  107.0 30.8 all-reduce.2
  140.0 49.9 all-gather.6
  191.4 35.7 all-gather.8
  453.8 58.7 reduce-scatter.1
